TPU v7x, 256 devices: a whole 4x4x8 slice. The times are simulated.
256 devices in a mesh: expert: 128 (over y_lo, z, x, core), dp: 2 (over y_hi).
Axes of the slice: x: 4, y: 4 (y_hi: 2, y_lo: 2; y = y_hi * 2 + y_lo), z: 8, core: 2. Of those that a mesh axis runs over, the one named last changes fastest.
Arguments:
- tokens: bfloat16 [32768, 2560], P(('expert', 'dp')), may hold values from -6 to 6
- routes: int32 [32768, 6], P(('expert', 'dp')), may hold values from 0 to 31, all different within a row; in each aligned block of 128 rows (0 to 127, 128 to 255, ...) at most 32 rows name the same one
- combine_weight: float32 [32768, 6], P(('expert', 'dp')), may hold values from 0.05 to 1
- owner_plan: int32 [32], replicated, may hold values from 0 to 31, as said below
- w_in: bfloat16 [2, 24576, 2560], P(None, 'expert', 'dp'), may hold values from -0.125 to 0.125
- w_out: bfloat16 [24576, 2560], P('expert', 'dp'), may hold values from -0.21875 to 0.21875
- grad_in: bfloat16 [2, 2, 24576, 2560], P('dp', None, 'expert'), may hold values from -6 to 6
- grad_out: bfloat16 [2, 24576, 2560], P('dp', 'expert'), may hold values from -6 to 6
- first_in: bfloat16 [2, 24576, 2560], P(None, 'expert', 'dp'), may hold values from -3 to 3
- second_in: bfloat16 [2, 24576, 2560], P(None, 'expert', 'dp'), may hold values from 0.25 to 4
- first_out: bfloat16 [24576, 2560], P('expert', 'dp'), may hold values from -3 to 3
- second_out: bfloat16 [24576, 2560], P('expert', 'dp'), may hold values from 0.25 to 4
Outputs:
- combined: bfloat16 [32768, 2560], P(('expert', 'dp'))
- first_in_next: bfloat16 [2, 24576, 2560], P(None, 'expert', 'dp')
- second_in_next: bfloat16 [2, 24576, 2560], P(None, 'expert', 'dp')
- first_out_next: bfloat16 [24576, 2560], P('expert', 'dp')
- second_out_next: bfloat16 [24576, 2560], P('expert', 'dp')
Inputs may be any that keep to these rules, and one draw needn't show every extreme that they name: owner_plan is an involution: exactly 4 pairs of experts trade owners, every other expert maps to itself. `routes`: in the rows of one device (128 rows) no expert is named by more than 32 rows, a bound that some expert reaches in some device.
All inputs are finite; a program needn't handle non-finite values.
Results may differ from a plain program's by a relative error of at most 0.014.
Values may be sent and summed in bfloat16 or wider, within the bound.
A program may use at most 192 MiB of HBM per device.

v0:
```python
import jax
import jax.numpy as jnp
from jax import lax
from jax.sharding import PartitionSpec as P

GROUP = 4


BETA_ONE = 0.9
BETA_TWO = 0.95
LEARNING_RATE = 0.005
EPSILON = 1e-08
CORRECT_FIRST = 1.0 / (1.0 - 0.9**10)
CORRECT_SECOND = 1.0 / (1.0 - 0.95**10)


def sent_together(arrays, axis, split_dim, concat_dim, along):
    both = jnp.concatenate(arrays, axis=along)
    result, at, outs = (
        lax.all_to_all(both, axis, split_axis=split_dim, concat_axis=concat_dim, tiled=True),
        0,
        [],
    )
    for a in arrays:
        outs.append(lax.slice_in_dim(result, at, at + a.shape[along], axis=along))
        at += a.shape[along]
    return tuple(outs)


def cut_along(shard, dim, devices):
    before, after = (shard.shape[:dim], shard.shape[dim + 1 :])
    return jnp.moveaxis(shard.reshape(*before, devices, -1, *after), dim, 0)


def sum_at_owner(shard, axis, dim):
    devices = lax.axis_size(axis)
    parts = lax.all_to_all(cut_along(shard, dim, devices), axis, 0, 0, tiled=True)
    return jnp.sum(parts.astype(jnp.float32), axis=0)


def swapped(shard, axis, distance):
    return lax.ppermute(shard, axis, [(i, i ^ 1 << distance) for i in range(lax.axis_size(axis))])


def adam_update(weight, gradient, first_moment, second_moment):
    first_next = BETA_ONE * first_moment.astype(jnp.float32) + (1.0 - BETA_ONE) * gradient
    second_next = (
        BETA_TWO * second_moment.astype(jnp.float32) + (1.0 - BETA_TWO) * gradient * gradient
    )
    stepped = weight.astype(jnp.float32) - LEARNING_RATE * (first_next * CORRECT_FIRST) / (
        jnp.sqrt(second_next * CORRECT_SECOND) + EPSILON
    )
    return (
        stepped.astype(jnp.bfloat16),
        first_next.astype(jnp.bfloat16),
        second_next.astype(jnp.bfloat16),
    )


def slot_ranks(flat_routes, expert_count):
    onehot = (flat_routes[:, None] == jnp.arange(expert_count, dtype=jnp.int32)[None, :]).astype(
        jnp.int32
    )
    ranks = jnp.cumsum(onehot, axis=0) - 1
    return jnp.sum(ranks * onehot, axis=1)


def times_rows(row_data, weight_rows):
    return lax.dot_general(
        row_data, weight_rows, (((1,), (1,)), ((), ())), preferred_element_type=jnp.float32
    )


def expert_rows(row_data, weight_in, weight_out):
    gate = times_rows(row_data, weight_in[0])
    upward = times_rows(row_data, weight_in[1])
    hidden = (jax.nn.silu(gate) * upward).astype(jnp.bfloat16)
    return jnp.dot(hidden, weight_out, preferred_element_type=jnp.float32).astype(jnp.bfloat16)


def migrate_weights(shard_in, shard_out, source_rows, device_count):
    spread_in, spread_out = sent_together(
        (shard_in.reshape(device_count, -1), shard_out.reshape(device_count, -1)), "expert", 0, 0, 1
    )
    picked_in = jnp.take(spread_in, source_rows, axis=0)
    picked_out = jnp.take(spread_out, source_rows, axis=0)
    landed_in, landed_out = sent_together((picked_in, picked_out), "expert", 0, 0, 1)
    return (landed_in.reshape(shard_in.shape), landed_out.reshape(shard_out.shape))


def migrate_moments(first_in, second_in, first_out, second_out, source_rows, device_count):
    spread = sent_together(
        (
            first_in.reshape(device_count, -1),
            second_in.reshape(device_count, -1),
            first_out.reshape(device_count, -1),
            second_out.reshape(device_count, -1),
        ),
        "expert",
        0,
        0,
        1,
    )
    picked = [jnp.take(block, source_rows, axis=0) for block in spread]
    landed = sent_together((picked[0], picked[1], picked[2], picked[3]), "expert", 0, 0, 1)
    return (
        landed[0].reshape(first_in.shape),
        landed[1].reshape(second_in.shape),
        landed[2].reshape(first_out.shape),
        landed[3].reshape(second_out.shape),
    )


def local(
    tokens,
    routes,
    combine_weight,
    owner_plan,
    w_in,
    w_out,
    grad_in,
    grad_out,
    first_in,
    second_in,
    first_out,
    second_out,
):
    device_count = lax.axis_size("expert")
    expert_count = device_count // GROUP
    token_count, route_count = routes.shape
    width = tokens.shape[1]
    capacity = GROUP * (
        (token_count * route_count * 4 + 3 * expert_count * GROUP - 1) // (3 * expert_count * GROUP)
    )
    summed_in, summed_out = (
        sum_at_owner(grad_in.astype(jnp.float32).astype(jnp.bfloat16), "dp", 3),
        sum_at_owner(grad_out.astype(jnp.float32).astype(jnp.bfloat16), "dp", 2),
    )
    new_in, first_in_next, second_in_next = adam_update(w_in, summed_in[0], first_in, second_in)
    new_out, first_out_next, second_out_next = adam_update(
        w_out, summed_out[0], first_out, second_out
    )
    device_ids = jnp.arange(device_count, dtype=jnp.int32)
    source_rows = jnp.take(owner_plan, device_ids // GROUP) * GROUP + device_ids % GROUP
    moved_in, moved_out = migrate_weights(new_in, new_out, source_rows, device_count)
    moments = migrate_moments(
        first_in_next, second_in_next, first_out_next, second_out_next, source_rows, device_count
    )
    full_in, full_out = (
        lax.all_gather(moved_in, "dp", axis=2, tiled=True),
        lax.all_gather(moved_out, "dp", axis=1, tiled=True),
    )
    flat_routes = routes.reshape(-1)
    ranks = slot_ranks(flat_routes, expert_count)
    targets = (flat_routes * capacity + ranks).reshape(token_count, route_count)
    slot_ids = jnp.arange(expert_count * capacity, dtype=jnp.int32)
    selector = jnp.any(targets[None, :, :] == slot_ids[:, None, None], axis=2).astype(jnp.bfloat16)
    by_expert = (
        jnp.dot(selector, tokens, preferred_element_type=jnp.float32)
        .astype(jnp.bfloat16)
        .reshape(expert_count, capacity, width)
    )
    by_group = jnp.take(by_expert, owner_plan, axis=0)
    share = capacity // GROUP
    my_slot = lax.axis_index("expert") % GROUP
    stacked = jnp.concatenate([full_in, full_out[None]], 0)
    for bit_index in range(GROUP.bit_length() - 1):
        partner = swapped(stacked, "expert", bit_index)
        is_lower = my_slot // (1 << bit_index) % 2 == 0
        stacked = jnp.where(
            is_lower, jnp.concatenate([stacked, partner], 1), jnp.concatenate([partner, stacked], 1)
        )
    quarter_rows = full_out.shape[0]
    send_rows = by_group.reshape(device_count, share, width)
    arrived = lax.all_to_all(send_rows, "expert", split_axis=0, concat_axis=0, tiled=True)
    flat_rows = arrived.reshape(-1, width)
    total = jnp.zeros((flat_rows.shape[0], width), jnp.float32)
    for quarter in range(GROUP):
        begin = quarter * quarter_rows
        block = stacked[:, begin : begin + quarter_rows]
        total = total + expert_rows(flat_rows, block[:2], block[2]).astype(jnp.float32)
    results = total.astype(jnp.bfloat16).reshape(arrived.shape)
    returned = lax.all_to_all(results, "expert", split_axis=0, concat_axis=0, tiled=True)
    by_group_out = returned.reshape(expert_count, capacity, width)
    by_expert_out = jnp.take(by_group_out, owner_plan, axis=0).reshape(
        expert_count * capacity, width
    )
    weight_table = jnp.sum(
        jnp.where(targets[:, :, None] == slot_ids[None, None, :], combine_weight[:, :, None], 0.0),
        axis=1,
    )
    weight_high = weight_table.astype(jnp.bfloat16)
    weight_low = (weight_table - weight_high.astype(jnp.float32)).astype(jnp.bfloat16)
    combined_sum = jnp.dot(
        weight_high, by_expert_out, preferred_element_type=jnp.float32
    ) + jnp.dot(weight_low, by_expert_out, preferred_element_type=jnp.float32)
    combined = combined_sum.astype(jnp.bfloat16)
    return (combined, moments[0], moments[1], moments[2], moments[3])


def solution(mesh):
    in_specs = (
        P(("expert", "dp"), None),
        P(("expert", "dp"), None),
        P(("expert", "dp"), None),
        P(),
        P(None, "expert", "dp"),
        P("expert", "dp"),
        P("dp", None, "expert", None),
        P("dp", "expert", None),
        P(None, "expert", "dp"),
        P(None, "expert", "dp"),
        P("expert", "dp"),
        P("expert", "dp"),
    )
    out_specs = (
        P(("expert", "dp"), None),
        P(None, "expert", "dp"),
        P(None, "expert", "dp"),
        P("expert", "dp"),
        P("expert", "dp"),
    )
    return jax.shard_map(local, mesh=mesh, in_specs=in_specs, out_specs=out_specs, check_vma=False)
```

profile of v0, /device:TPU:1, one launch (start us, length us, event | category | flops | bytes accessed | tf_op | source)
XLA Modules:
  0.0 794.4 jit_solution(18260944956797738191)
XLA Ops:
  10.8 5.0 all-to-all-start.2
  15.8 4.3 reshape.182
  21.6 6.6 all-to-all-done.2
  28.2 3.7 all-to-all-start.1
  33.4 3.1 fusion.23
  37.6 16.1 %all-to-all-done.1 = bf16[2,1,2,192,1280]{4,3,2,1,0:T(8,128)(2,1)S(1)} async-done(((bf16[2,1,2,192,1280]{4,3,2,1,0:T(8,128)(2,1)}), bf16[2,1,2,192,1280]{4,3,2,1,0:T(8,128)(2,1)S(1)}, u32[]{:S(2)}, u32[]{:S(2)}) %all-to-all-start.1) | async-done | bytes 1966112 | tf_op jit(solution)/shard_map/all_to_all | solution.py:37
  54.0 4.4 fusion.20
  64.3 4.7 reshape.296
  68.9 19.2 %all-to-all-start.3 = ((bf16[128,2,2880]{2,1,0:T(2,128)(2,1)}), bf16[128,2,2880]{2,1,0:T(2,128)(2,1)S(1)}, u32[]{:S(2)}, u32[]{:S(2)}) async-start(bf16[128,2,2880]{2,1,0:T(2,128)(2,1)} %reshape.296), calls=%async_computation.3 | async-start | bytes 3014656 | tf_op jit(solution)/shard_map/all_to_all | solution.py:20
  96.1 3.1 maximum_bitcast_fusion
  99.2 5.5 reduce.4
  104.7 6.8 reshape.300
  111.5 18.0 %all-to-all-done.3 = bf16[128,2,2880]{2,1,0:T(2,128)(2,1)S(1)} async-done(((bf16[128,2,2880]{2,1,0:T(2,128)(2,1)}), bf16[128,2,2880]{2,1,0:T(2,128)(2,1)S(1)}, u32[]{:S(2)}, u32[]{:S(2)}) %all-to-all-start.3) | async-done | bytes 1474592 | tf_op jit(solution)/shard_map/all_to_all | solution.py:20
  129.5 6.8 all-to-all-start.6
  137.7 4.2 reshape.297
  147.9 58.6 %all-to-all-done.6 = bf16[128,2,5760]{2,1,0:T(2,128)(2,1)} async-done(((bf16[128,2,5760]{2,1,0:T(2,128)(2,1)}), bf16[128,2,5760]{2,1,0:T(2,128)(2,1)}, u32[]{:S(2)}, u32[]{:S(2)}) %all-to-all-start.6) | async-done | bytes 2949152 | tf_op jit(solution)/shard_map/all_to_all | solution.py:20
  206.5 18.8 %reshape.301 = bf16[128,1,11520]{2,1,0:T(2,128)(2,1)} reshape(bf16[128,2,5760]{2,1,0:T(2,128)(2,1)} %all-to-all-done.6) | data formatting | bytes 5898240
  244.6 4.7 reshape.298
  249.2 5.3 all-to-all-start.4
  257.6 38.3 %all-to-all-done.4 = bf16[128,2,2880]{2,1,0:T(2,128)(2,1)S(1)} async-done(((bf16[128,2,2880]{2,1,0:T(2,128)(2,1)}), bf16[128,2,2880]{2,1,0:T(2,128)(2,1)S(1)}, u32[]{:S(2)}, u32[]{:S(2)}) %all-to-all-start.4) | async-done | bytes 1474592 | tf_op jit(solution)/shard_map/all_to_all | solution.py:20
  295.8 4.2 reshape.299
  305.9 3.8 convolution_convert_fusion.4
  309.7 6.1 gather_fusion.1
  315.8 5.4 broadcast_select_fusion
  321.2 6.5 all-to-all-start
  328.0 42.7 %all_gather.7 = bf16[192,2560]{1,0:T(8,128)(2,1)S(1)} all-gather(bf16[192,1280]{1,0:T(8,128)(2,1)S(1)} %reshape.187), channel_id=1, replica_groups=mesh['expert'=128,'dp'=2] {'dp'}, dimensions={1}, use_global_device_ids=true | all-gather | bytes 1474560 | tf_op jit(solution)/shard_map/all_gather | solution.py:151
  370.7 3.4 pad_maximum_fusion
  374.4 5.5 collective-permute-done
  379.9 7.3 maximum_select_fusion.1
  387.1 4.6 collective-permute-start.1
  394.6 5.4 reduce.7
  400.0 6.8 reshape.302
  406.8 39.5 %all-to-all-done = bf16[128,8,2560]{2,1,0:T(8,128)(2,1)} async-done(((bf16[128,8,2560]{2,1,0:T(8,128)(2,1)}), bf16[128,8,2560]{2,1,0:T(8,128)(2,1)}, u32[]{:S(2)}, u32[]{:S(2)}) %all-to-all-start) | async-done | bytes 5242912 | tf_op jit(solution)/shard_map/all_to_all | solution.py:175
  446.3 6.4 all-to-all-start.7
  452.7 117.1 %collective-permute-done.1 = bf16[3,384,2560]{2,1,0:T(8,128)(2,1)} collective-permute-done((bf16[3,384,2560]{2,1,0:T(8,128)(2,1)}, bf16[3,384,2560]{2,1,0:T(8,128)(2,1)}, u32[]{:S(2)}, u32[]{:S(2)}) %collective-permute-start.1) | collective-permute-done | bytes 5898272 | tf_op jit(solution)/shard_map/ppermute | solution.py:42
  569.8 10.0 %maximum_select_fusion = bf16[3,768,2560]{2,1,0:T(8,128)(2,1)S(1)} fusion(bf16[3,384,2560]{2,1,0:T(8,128)(2,1)} %collective-permute-done.1, bf16[3,384,2560]{2,1,0:T(8,128)(2,1)} %maximum_select_fusion.1, pred[]{:T(512)S(6)} %eq.77), kind=kLoop, calls=%fused_computation.9 | loop fusion | flops 53084160 | bytes 23592960 | tf_op jit(solution)/shard_map/jit(_where)/select_n | solution.py:170
  579.9 9.1 %fusion.13 = f32[1024,192]{0,1:T(8,128)} fusion(bf16[128,8,2560]{2,1,0:T(8,128)(2,1)} %all-to-all-done, bf16[3,768,2560]{2,1,0:T(8,128)(2,1)S(1)} %maximum_select_fusion), kind=kOutput, calls=%fused_computation.30 | convolution fusion | flops 1006632960 | bytes 7012352 | tf_op jit(solution)/shard_map/dot_general | solution.py:69
  588.9 4.3 fusion.9
  593.3 4.3 fusion.5
  597.6 4.3 fusion.1
  601.9 9.0 %convolution_convert_fusion.3 = bf16[1024,2560]{1,0:T(8,128)(2,1)} fusion(bf16[3,768,2560]{2,1,0:T(8,128)(2,1)} %copy-done.4, f32[1024,192]{0,1:T(8,128)} %fusion.13, bf16[128,8,2560]{2,1,0:T(8,128)(2,1)} %all-to-all-done), kind=kOutput, calls=%fused_computation.15 | convolution fusion | flops 2017067008 | bytes 13238272 | tf_op jit(solution)/shard_map/dot_general | solution.py:78
  610.9 8.7 %convolution_convert_fusion.2 = bf16[1024,2560]{1,0:T(8,128)(2,1)} fusion(bf16[3,768,2560]{2,1,0:T(8,128)(2,1)} %copy-done.4, f32[1024,192]{0,1:T(8,128)S(1)} %fusion.9, bf16[128,8,2560]{2,1,0:T(8,128)(2,1)} %all-to-all-done), kind=kOutput, calls=%fused_computation.14 | convolution fusion | flops 2017067008 | bytes 13238272 | tf_op jit(solution)/shard_map/dot_general | solution.py:78
  619.7 8.8 %convolution_convert_fusion.1 = bf16[1024,2560]{1,0:T(8,128)(2,1)} fusion(bf16[3,768,2560]{2,1,0:T(8,128)(2,1)} %copy-done.4, f32[1024,192]{0,1:T(8,128)S(1)} %fusion.5, bf16[128,8,2560]{2,1,0:T(8,128)(2,1)} %all-to-all-done), kind=kOutput, calls=%fused_computation.13 | convolution fusion | flops 2017067008 | bytes 13238272 | tf_op jit(solution)/shard_map/dot_general | solution.py:78
  628.4 14.4 %fusion = bf16[128,8,2560]{2,1,0:T(8,128)(2,1)} fusion(bf16[1024,2560]{1,0:T(8,128)(2,1)} %convolution_convert_fusion.1, bf16[1024,2560]{1,0:T(8,128)(2,1)} %convolution_convert_fusion.2, bf16[1024,2560]{1,0:T(8,128)(2,1)} %convolution_convert_fusion.3, bf16[3,768,2560]{2,1,0:T(8,128)(2,1)} %copy-done.4, f32[1024,192]{0,1:T(8,128)S(1)} %fusion.1, ...), kind=kOutput, calls=%fused_computation.17 | convolution fusion | flops 2038038528 | bytes 28966912 | tf_op jit(solution)/shard_map/dot_general | solution.py:78
  642.8 13.0 %all-to-all-start.5 = ((bf16[128,8,2560]{2,1,0:T(8,128)(2,1)}), bf16[128,8,2560]{2,1,0:T(8,128)(2,1)}, u32[]{:S(2)}, u32[]{:S(2)}) async-start(bf16[128,8,2560]{2,1,0:T(8,128)(2,1)} %fusion), calls=%async_computation.5 | async-start | bytes 10485760 | tf_op jit(solution)/shard_map/all_to_all | solution.py:183
  656.3 18.8 %reshape.303 = bf16[128,1,11520]{2,1,0:T(2,128)(2,1)} reshape(bf16[128,2,5760]{2,1,0:T(2,128)(2,1)} %all-to-all-done.7) | data formatting | bytes 5898240
  686.0 89.8 %all-to-all-done.5 = bf16[128,8,2560]{2,1,0:T(8,128)(2,1)} async-done(((bf16[128,8,2560]{2,1,0:T(8,128)(2,1)}), bf16[128,8,2560]{2,1,0:T(8,128)(2,1)}, u32[]{:S(2)}, u32[]{:S(2)}) %all-to-all-start.5) | async-done | bytes 5242912 | tf_op jit(solution)/shard_map/all_to_all | solution.py:183
  775.8 5.7 gather_fusion.4
  (98 shorter events, 77.5 us)
Async XLA Ops:
  7.2 298.7 %copy-start = (bf16[128,2560]{1,0:T(8,128)(2,1)S(1)}, bf16[128,2560]{1,0:T(8,128)(2,1)}, u32[]{:S(2)}) copy-start(bf16[128,2560]{1,0:T(8,128)(2,1)} %param.18) | copy-start | bytes 1966084
  10.8 17.3 %all-to-all-start.2 = ((bf16[2,1,192,1280]{3,2,1,0:T(8,128)(2,1)}), bf16[2,1,192,1280]{3,2,1,0:T(8,128)(2,1)}, u32[]{:S(2)}, u32[]{:S(2)}) async-start(bf16[2,1,192,1280]{3,2,1,0:T(8,128)(2,1)} %copy.64), calls=%async_computation.2 | async-start | bytes 1966080 | tf_op jit(solution)/shard_map/all_to_all | solution.py:37
  28.2 25.5 %all-to-all-start.1 = ((bf16[2,1,2,192,1280]{4,3,2,1,0:T(8,128)(2,1)}), bf16[2,1,2,192,1280]{4,3,2,1,0:T(8,128)(2,1)S(1)}, u32[]{:S(2)}, u32[]{:S(2)}) async-start(bf16[2,1,2,192,1280]{4,3,2,1,0:T(8,128)(2,1)} %copy.63), calls=%async_computation.1 | async-start | bytes 3932160 | tf_op jit(solution)/shard_map/all_to_all | solution.py:37
  68.9 60.6 %all-to-all-start.3 = ((bf16[128,2,2880]{2,1,0:T(2,128)(2,1)}), bf16[128,2,2880]{2,1,0:T(2,128)(2,1)S(1)}, u32[]{:S(2)}, u32[]{:S(2)}) async-start(bf16[128,2,2880]{2,1,0:T(2,128)(2,1)} %reshape.296), calls=%async_computation.3 | async-start | bytes 3014656 | tf_op jit(solution)/shard_map/all_to_all | solution.py:20
  104.7 31.7 %copy-start.2 = (s32[32]{0:T(128)S(1)}, s32[32]{0:T(128)}, u32[]{:S(2)}) copy-start(s32[32]{0:T(128)} %param.21) | copy-start | bytes 388
  129.5 76.9 %all-to-all-start.6 = ((bf16[128,2,5760]{2,1,0:T(2,128)(2,1)}), bf16[128,2,5760]{2,1,0:T(2,128)(2,1)}, u32[]{:S(2)}, u32[]{:S(2)}) async-start(bf16[128,2,5760]{2,1,0:T(2,128)(2,1)} %reshape.300), calls=%async_computation.6 | async-start | bytes 5898240 | tf_op jit(solution)/shard_map/all_to_all | solution.py:20
  231.3 2.1 copy-start.3
  233.5 3.4 copy-start.6
  236.9 2.9 copy-start.9
  236.9 2.9 copy-start.10
  242.0 12.8 %copy-start.11 = (s32[128,6]{0,1:T(8,128)S(1)}, s32[128,6]{0,1:T(8,128)}, u32[]{:S(2)}) copy-start(s32[128,6]{0,1:T(8,128)} %param.19) | copy-start | bytes 9220
  249.2 46.6 %all-to-all-start.4 = ((bf16[128,2,2880]{2,1,0:T(2,128)(2,1)}), bf16[128,2,2880]{2,1,0:T(2,128)(2,1)S(1)}, u32[]{:S(2)}, u32[]{:S(2)}) async-start(bf16[128,2,2880]{2,1,0:T(2,128)(2,1)} %reshape.298), calls=%async_computation.4 | async-start | bytes 3014656 | tf_op jit(solution)/shard_map/all_to_all | solution.py:20
  254.6 116.2 %all-gather.2.cloned.1.call-start = ((), (), s32[]{:S(2)}) async-start(), calls=%async_computation.8 | async-start | bytes 2949120 | tf_op jit(solution)/shard_map/all_gather | solution.py:150
  321.2 125.1 %all-to-all-start = ((bf16[128,8,2560]{2,1,0:T(8,128)(2,1)}), bf16[128,8,2560]{2,1,0:T(8,128)(2,1)}, u32[]{:S(2)}, u32[]{:S(2)}) async-start(bf16[128,8,2560]{2,1,0:T(8,128)(2,1)} %bitcast.141), calls=%async_computation | async-start | bytes 10485760 | tf_op jit(solution)/shard_map/all_to_all | solution.py:175
  374.1 5.7 collective-permute-start
  374.4 17.4 %copy-start.7 = (bf16[128,1920]{1,0:T(8,128)(2,1)S(1)}, bf16[128,1920]{1,0:T(8,128)(2,1)}, u32[]{:S(2)}) copy-start(bf16[128,1920]{1,0:T(8,128)(2,1)} %get-tuple-element.27) | copy-start | bytes 1474564
  374.4 17.4 %copy-start.8 = (bf16[128,1920]{1,0:T(8,128)(2,1)S(1)}, bf16[128,1920]{1,0:T(8,128)(2,1)}, u32[]{:S(2)}) copy-start(bf16[128,1920]{1,0:T(8,128)(2,1)} %get-tuple-element.28) | copy-start | bytes 1474564
  387.1 182.7 %collective-permute-start.1 = (bf16[3,384,2560]{2,1,0:T(8,128)(2,1)}, bf16[3,384,2560]{2,1,0:T(8,128)(2,1)}, u32[]{:S(2)}, u32[]{:S(2)}) collective-permute-start(bf16[3,384,2560]{2,1,0:T(8,128)(2,1)} %maximum_select_fusion.1), channel_id=1, source_target_pairs={{0,4},{2,6},{4,0},{6,2},{8,12},{10,14},{12,8},{14,10},{16,20},{18,... | collective-permute-start | bytes 17694728 | tf_op jit(solution)/shard_map/ppermute | solution.py:42
  446.3 196.5 %all-to-all-start.7 = ((bf16[128,2,5760]{2,1,0:T(2,128)(2,1)}), bf16[128,2,5760]{2,1,0:T(2,128)(2,1)}, u32[]{:S(2)}, u32[]{:S(2)}) async-start(bf16[128,2,5760]{2,1,0:T(2,128)(2,1)} %reshape.302), calls=%async_computation.7 | async-start | bytes 5898240 | tf_op jit(solution)/shard_map/all_to_all | solution.py:20
  579.8 17.8 %copy-start.4 = (bf16[3,768,2560]{2,1,0:T(8,128)(2,1)}, bf16[3,768,2560]{2,1,0:T(8,128)(2,1)S(1)}, u32[]{:S(2)}) copy-start(bf16[3,768,2560]{2,1,0:T(8,128)(2,1)S(1)} %maximum_select_fusion) | copy-start | bytes 35389444
  642.8 13.0 %copy-start.12 = (f32[128,6]{0,1:T(8,128)S(1)}, f32[128,6]{0,1:T(8,128)}, u32[]{:S(2)}) copy-start(f32[128,6]{0,1:T(8,128)} %param.20) | copy-start | bytes 9220
  642.8 133.0 %all-to-all-start.5 = ((bf16[128,8,2560]{2,1,0:T(8,128)(2,1)}), bf16[128,8,2560]{2,1,0:T(8,128)(2,1)}, u32[]{:S(2)}, u32[]{:S(2)}) async-start(bf16[128,8,2560]{2,1,0:T(8,128)(2,1)} %fusion), calls=%async_computation.5 | async-start | bytes 10485760 | tf_op jit(solution)/shard_map/all_to_all | solution.py:183
  678.1 1.6 copy-start.5
  784.5 2.6 copy-start.1
Sparse Core Ops, SparseCore 0:
  305.5 57.3 all-gather.1
where the time goes:
time: 806 us; the launch traced here: 794 us
  waiting for transfers between devices  389 us (48%)
  local copies, waits for them, and re-layouts  137 us (17%)
  starting transfers between devices  71.1 us (9%)
  other arithmetic  69.7 us (9%)
  matrix products  69.3 us (9%)
  blocking collectives  42.7 us (5%)
  between operations  14.9 us (2%)
    ppermute x2, waiting for transfers between devices, swapped(): lax.ppermute(shard, axis, [(i, i ^ 1 << distance) for i in range(lax.axis...  123 us
    all_to_all x4, waiting for transfers between devices, sent_together(): lax.all_to_all(both, axis, split_axis=split_dim, concat_axis=concat_dim,...  115 us
    all_to_all x1, waiting for transfers between devices, local(): lax.all_to_all(results, 'expert', split_axis=0, concat_axis=0, tiled=True)  89.8 us
    unnamed x39, local copies, waits for them, and re-layouts  80.8 us
    all_gather x1, blocking collectives, local(): lax.all_gather(moved_out, 'dp', axis=1, tiled=True)  42.7 us
    dot_general x4, matrix products, expert_rows(): jnp.dot(hidden, weight_out, preferred_element_type=jnp.float32)  40.9 us
    all_to_all x1, waiting for transfers between devices, local(): lax.all_to_all(send_rows, 'expert', split_axis=0, concat_axis=0, tiled=True)  39.5 us
    all_to_all x4, starting transfers between devices, sent_together(): lax.all_to_all(both, axis, split_axis=split_dim, concat_axis=concat_dim,...  37.8 us
  transfers between devices with their start and end apart: 11, of which 9 were waited for; matrix products, arithmetic and copies ran while one was open for 24% of the time, Pallas kernels for 0%

commit v1 on v0

v1 whole, which is shorter than its diff:
```python
import functools
import jax
import jax.numpy as jnp
from jax import lax
from jax.experimental import pallas as pl
from jax.experimental.pallas import tpu as pltpu
from jax.sharding import Mesh, PartitionSpec as P

BETA_ONE = 0.9
BETA_TWO = 0.95
LEARNING_RATE = 0.005
EPSILON = 1e-08
CORRECT_FIRST = 1.0 / (1.0 - 0.9**10)
CORRECT_SECOND = 1.0 / (1.0 - 0.95**10)
CAP = 32
PLANE = 4
EXTRA = 128
EX = ("yl", "z", "xh", "xl", "c")
MESH = pl.DeviceIdType.MESH


def at_x(v):
    return {"xh": v // 2, "xl": v % 2}


def at_y(v):
    return {"dp": v // 2, "yl": v % 2}


def at_z(v):
    return {"z": v}


def place():
    x = lax.axis_index("xh") * 2 + lax.axis_index("xl")
    y = lax.axis_index("dp") * 2 + lax.axis_index("yl")
    return x, y, lax.axis_index("z"), lax.axis_index("c")


def greet(peers):
    barrier = pltpu.get_barrier_semaphore()
    for peer in peers:
        pl.semaphore_signal(barrier, inc=1, device_id=peer, device_id_type=MESH)
    pl.semaphore_wait(barrier, len(peers))


class Copies:
    def __init__(self, send_sems, recv_sems):
        self.send_sems, self.recv_sems, self.made = send_sems, recv_sems, []

    def send(self, src, dst, peer):
        i = len(self.made)
        copy = pltpu.make_async_remote_copy(
            src_ref=src,
            dst_ref=dst,
            send_sem=self.send_sems.at[i],
            recv_sem=self.recv_sems.at[i],
            device_id=peer,
            device_id_type=MESH,
        )
        copy.start()
        self.made.append(copy)
        return copy

    def finish(self):
        for copy in self.made:
            copy.wait_send()


N_GATHER = 40 + 8 + 9


def gather_kernel(tok_ref, w_ref, tok_out, w_out, send_sems, recv_sems, own_sems):
    x, y, z, c = place()
    xr, xl = (x + 1) % 4, (x + 3) % 4
    yr, yl = (y + 1) % 4, (y + 3) % 4
    zr, zl = (z + 1) % 8, (z + 7) % 8
    greet([at_x(xr), at_x(xl), at_y(yr), at_y(yl), at_z(zr), at_z(zl), {"c": 1 - c}])
    cs = Copies(send_sems, recv_sems)
    rows = w_ref.shape[1]
    h, q = rows // 2, rows // 4
    t = tok_ref.shape[0]

    def weights(slot, start, size):
        return w_out.at[slot, :, pl.ds(start, size)]

    def ring(base, slot_src, slot_of, peer_of, mine, src=None):
        right, left = (mine + 1) % 4, (mine + 3) % 4
        held = weights(slot_src, base, h) if src is None else src
        a = cs.send(held, weights(slot_src, base, h), peer_of(right))
        b = cs.send(held, weights(slot_src, base, h), peer_of(left))

        def forward():
            a.wait_recv()
            f = cs.send(
                weights(slot_of(left), base, q), weights(slot_of(left), base, q), peer_of(right)
            )
            b.wait_recv()
            g = cs.send(
                weights(slot_of(right), base + q, q),
                weights(slot_of(right), base + q, q),
                peer_of(left),
            )
            return f, g

        return forward

    def slot(yy, xx):
        return yy * 4 + xx

    own = slot(y, x)
    own_w = pltpu.make_async_copy(w_ref, w_out.at[own], own_sems.at[0])
    own_t = pltpu.make_async_copy(tok_ref, tok_out.at[z * 2 + c], own_sems.at[1])
    own_w.start()
    own_t.start()

    def x_ring(base, yy, src=None):
        return ring(base, slot(yy, x), lambda v: slot(yy, v), at_x, x, src)

    def y_ring(base, xx, src=None):
        return ring(base, slot(y, xx), lambda v: slot(v, xx), at_y, y, src)

    part_a, part_b = w_ref.at[:, pl.ds(0, h)], w_ref.at[:, pl.ds(h, h)]
    a1 = x_ring(0, y, part_a)
    b1 = y_ring(h, x, part_b)

    def tokens(place_z, half=None, core=c):
        ref = tok_out.at[place_z * 2 + core]
        return ref if half is None else ref.at[pl.ds(half * (t // 2), t // 2)]

    partner = {"c": 1 - c}
    t_r = cs.send(tok_ref, tokens(z), at_z(zr))
    t_l = cs.send(tok_ref, tokens(z), at_z(zl))
    kept = [cs.send(tok_ref, tokens(z), partner)]
    a2 = [y_ring(0, x, part_a)]
    b2 = [x_ring(h, y, part_b)]

    def token_step(s, last):
        nonlocal t_r, t_l
        from_l, from_r = (z + 8 - s) % 8, (z + s) % 8
        t_r.wait_recv()
        half = 0 if last else None
        n_r = cs.send(tokens(from_l, half), tokens(from_l, half), at_z(zr))
        t_l.wait_recv()
        half = 1 if last else None
        n_l = cs.send(tokens(from_r, half), tokens(from_r, half), at_z(zl))
        kept.append(cs.send(tokens(from_l), tokens(from_l), partner))
        kept.append(cs.send(tokens(from_r), tokens(from_r), partner))
        t_r, t_l = n_r, n_l

    f, g = a1()
    a2.append(y_ring(0, xl))
    a2.append(y_ring(0, xr))
    u, v = b1()
    b2.append(x_ring(h, yl))
    b2.append(x_ring(h, yr))
    token_step(1, False)
    f.wait_recv()
    g.wait_recv()
    a2.append(y_ring(0, (x + 2) % 4))
    u.wait_recv()
    v.wait_recv()
    b2.append(x_ring(h, (y + 2) % 4))
    ends = []
    ends += a2[0]()
    ends += b2[0]()
    token_step(2, False)
    ends += a2[1]()
    ends += b2[1]()
    token_step(3, True)
    ends += a2[2]()
    ends += b2[2]()
    t_r.wait_recv()
    t_l.wait_recv()
    far = (z + 4) % 8
    kept.append(cs.send(tokens(far, 0), tokens(far, 0), partner))
    kept.append(cs.send(tokens(far, 1), tokens(far, 1), partner))
    ends += a2[3]()
    ends += b2[3]()
    for copy in ends + kept:
        copy.wait_recv()
    cs.finish()
    own_w.wait()
    own_t.wait()


def gather_all(tok, w):
    sent = (w.size * 8 + tok.size * 4) * 2
    return pl.pallas_call(
        gather_kernel,
        out_shape=(
            jax.ShapeDtypeStruct((16, *tok.shape), tok.dtype),
            jax.ShapeDtypeStruct((16, *w.shape), w.dtype),
        ),
        in_specs=[pl.BlockSpec(memory_space=pltpu.HBM)] * 2,
        out_specs=(pl.BlockSpec(memory_space=pltpu.HBM),) * 2,
        scratch_shapes=[
            pltpu.SemaphoreType.DMA((N_GATHER + 2,)),
            pltpu.SemaphoreType.DMA((N_GATHER + 2,)),
            pltpu.SemaphoreType.DMA((2,)),
        ],
        compiler_params=pltpu.CompilerParams(collective_id=0, has_side_effects=True),
        cost_estimate=pl.CostEstimate(flops=0, bytes_accessed=400_000_000, transcendentals=0),
        name="gather_all",
    )(tok, w)


def moe_kernel(tok_ref, w_ref, out_ref, x_ref, slots_ref, weights_ref, *, width, top):
    j = pl.program_id(0)
    blocks, t = tok_ref.shape[0], tok_ref.shape[1]
    half = width // 2
    slots = PLANE * CAP

    @pl.when(j == 0)
    def _():
        z = lax.axis_index("z")
        lane = lax.broadcasted_iota(jnp.int32, (t, slots), 1)
        expert = (lane // (2 * CAP)) * 16 + z * 2 + (lane // CAP) % 2
        place_in = (expert * CAP + lane % CAP).astype(jnp.float32)

        def dispatch(b, _):
            info = tok_ref[b, :, width:].astype(jnp.float32)
            hit_any = jnp.zeros((t, slots), jnp.float32)
            total = jnp.zeros((t, slots), jnp.float32)
            for k in range(top):
                goal = info[:, k : k + 1] * CAP + info[:, top + k : top + k + 1]
                w = (
                    info[:, 2 * top + k : 2 * top + k + 1]
                    + info[:, 3 * top + k : 3 * top + k + 1]
                    + info[:, 4 * top + k : 4 * top + k + 1]
                )
                hit = goal == place_in
                hit_any = jnp.where(hit, 1.0, hit_any)
                total = jnp.where(hit, w, total)
            high = total.astype(jnp.bfloat16)
            low = (total - high.astype(jnp.float32)).astype(jnp.bfloat16)
            weights_ref[b] = jnp.concatenate([high, low], 1)
            rows = lax.dot_general(
                hit_any.astype(jnp.bfloat16),
                tok_ref[b, :, :width],
                (((0,), (0,)), ((), ())),
                preferred_element_type=jnp.float32,
            ).astype(jnp.bfloat16)
            for e in range(PLANE):
                x_ref[e, pl.ds(b * CAP, CAP), :] = rows[e * CAP : (e + 1) * CAP]
            return 0

        lax.fori_loop(0, blocks, dispatch, 0)

    dims = (((1,), (1,)), ((), ()))

    def chunk(m, _):
        mrows = 256
        at = pl.ds(m * mrows, mrows)
        x0, x1 = x_ref[j, at, :half], x_ref[j, at, half:]
        hidden = []
        for q in range(2):
            both = lax.dot_general(
                x0, w_ref[0, 0, 0, q, : 2 * 192], dims, preferred_element_type=jnp.float32
            ) + lax.dot_general(
                x1, w_ref[1, 0, 0, q, : 2 * 192], dims, preferred_element_type=jnp.float32
            )
            gate, up = both[:, :192], both[:, 192:]
            hidden.append((jax.nn.silu(gate) * up).astype(jnp.bfloat16))
        for d in range(2):
            out = jnp.dot(
                hidden[0], w_ref[d, 0, 0, 0, 2 * 192 :], preferred_element_type=jnp.float32
            ) + jnp.dot(
                hidden[1], w_ref[d, 0, 0, 1, 2 * 192 :], preferred_element_type=jnp.float32
            )
            x_ref[j, at, d * half : (d + 1) * half] = out.astype(jnp.bfloat16)
        return 0

    lax.fori_loop(0, blocks * CAP // 256, chunk, 0)

    @pl.when(j == PLANE - 1)
    def _():
        def combine(b, _):
            y = jnp.concatenate(
                [x_ref[e, pl.ds(b * CAP, CAP), :] for e in range(PLANE)], 0
            )
            y2 = jnp.concatenate([y, y], 0)
            out_ref[b] = jnp.dot(
                weights_ref[b], y2, preferred_element_type=jnp.float32
            ).astype(jnp.bfloat16)
            return 0

        lax.fori_loop(0, blocks, combine, 0)


def experts(all_tok, all_w, width, top):
    blocks, t, ext = all_tok.shape
    w = all_w.reshape(2, 2, 2, 2, 576, width // 2)
    whole = pl.BlockSpec(memory_space=pltpu.VMEM)
    return pl.pallas_call(
        functools.partial(moe_kernel, width=width, top=top),
        out_shape=jax.ShapeDtypeStruct((blocks, t, width), jnp.bfloat16),
        grid=(PLANE,),
        in_specs=[
            whole,
            pl.BlockSpec((2, 1, 1, 2, 576, width // 2), lambda j: (0, j // 2, j % 2, 0, 0, 0)),
        ],
        out_specs=whole,
        scratch_shapes=[
            pltpu.VMEM((PLANE, blocks * CAP, width), jnp.bfloat16),
            pltpu.VMEM((blocks, 8, 128), jnp.bfloat16),
            pltpu.VMEM((blocks, t, 2 * PLANE * CAP), jnp.bfloat16),
        ],
        compiler_params=pltpu.CompilerParams(vmem_limit_bytes=63 * 1024 * 1024),
        cost_estimate=pl.CostEstimate(
            flops=12_000_000_000, bytes_accessed=60_000_000, transcendentals=0
        ),
        name="experts",
    )(all_tok, w)


def add(a, b):
    return (a.astype(jnp.float32) + b.astype(jnp.float32)).astype(jnp.bfloat16)


N_SCATTER = 8 + 14


def scatter_kernel(p_ref, out_ref, cx, rr, rl, send_sems, recv_sems):
    x, y, z, c = place()
    zr, zl = (z + 1) % 8, (z + 7) % 8
    partner = {"c": 1 - c}
    greet([at_z(zr), at_z(zl), partner])
    cs = Copies(send_sems, recv_sems)
    t = out_ref.shape[0]
    h = t // 2
    order = [4, 3, 5, 2, 6, 1, 7, 0]
    swaps = {}
    for s in order:
        d = (z + s) % 8
        swaps[s] = cs.send(p_ref.at[d * 2 + (1 - c)], cx.at[s], partner)

    def own(s, rows):
        d = (z + s) % 8
        return add(p_ref[d * 2 + c, rows, :], cx[s, rows, :])

    low, high = pl.ds(0, h), pl.ds(h, h)
    swaps[4].wait_recv()
    cx[4, low, :] = own(4, low)
    far_r = cs.send(cx.at[4, low], rr.at[3, low], at_z(zr))
    cx[4, high, :] = own(4, high)
    far_l = cs.send(cx.at[4, high], rl.at[3, high], at_z(zl))
    swaps[3].wait_recv()
    swaps[5].wait_recv()
    cx[3, high, :] = own(3, high)
    r_high = cs.send(cx.at[3, high], rr.at[2, high], at_z(zr))
    cx[5, low, :] = own(5, low)
    l_low = cs.send(cx.at[5, low], rl.at[2, low], at_z(zl))
    r_low, l_high = far_r, far_l
    cx[3, low, :] = own(3, low)
    cx[5, high, :] = own(5, high)
    r_low.wait_recv()
    rr[3, low, :] = add(rr[3, low, :], cx[3, low, :])
    r_low = cs.send(rr.at[3, low], rr.at[2, low], at_z(zr))
    l_high.wait_recv()
    rl[3, high, :] = add(rl[3, high, :], cx[5, high, :])
    l_high = cs.send(rl.at[3, high], rl.at[2, high], at_z(zl))
    for s in (2, 1):
        swaps[s].wait_recv()
        swaps[8 - s].wait_recv()
        cx[s] = add(p_ref[((z + s) % 8) * 2 + c], cx[s])
        cx[8 - s] = add(p_ref[((z + 8 - s) % 8) * 2 + c], cx[8 - s])
        r_high.wait_recv()
        rr[s, high, :] = add(rr[s, high, :], cx[s, high, :])
        r_high = cs.send(rr.at[s, high], rr.at[s - 1, high], at_z(zr))
        l_low.wait_recv()
        rl[s, low, :] = add(rl[s, low, :], cx[8 - s, low, :])
        l_low = cs.send(rl.at[s, low], rl.at[s - 1, low], at_z(zl))
        r_low.wait_recv()
        rr[s, low, :] = add(rr[s, low, :], cx[s, low, :])
        r_low = cs.send(rr.at[s, low], rr.at[s - 1, low], at_z(zr))
        l_high.wait_recv()
        rl[s, high, :] = add(rl[s, high, :], cx[8 - s, high, :])
        l_high = cs.send(rl.at[s, high], rl.at[s - 1, high], at_z(zl))
    swaps[0].wait_recv()
    r_high.wait_recv()
    l_low.wait_recv()
    r_low.wait_recv()
    l_high.wait_recv()
    out_ref[...] = (
        p_ref[z * 2 + c].astype(jnp.float32)
        + cx[0].astype(jnp.float32)
        + rr[0].astype(jnp.float32)
        + rl[0].astype(jnp.float32)
    ).astype(jnp.bfloat16)
    cs.finish()


def scatter_sum(partial):
    blocks, t, width = partial.shape
    whole = pl.BlockSpec(memory_space=pltpu.VMEM)
    return pl.pallas_call(
        scatter_kernel,
        out_shape=jax.ShapeDtypeStruct((t, width), partial.dtype),
        in_specs=[whole],
        out_specs=whole,
        scratch_shapes=[
            pltpu.VMEM((8, t, width), jnp.bfloat16),
            pltpu.VMEM((4, t, width), jnp.bfloat16),
            pltpu.VMEM((4, t, width), jnp.bfloat16),
            pltpu.SemaphoreType.DMA((N_SCATTER,)),
            pltpu.SemaphoreType.DMA((N_SCATTER,)),
        ],
        compiler_params=pltpu.CompilerParams(
            collective_id=1, has_side_effects=True, vmem_limit_bytes=48 * 1024 * 1024
        ),
        cost_estimate=pl.CostEstimate(flops=0, bytes_accessed=200_000_000, transcendentals=0),
        name="scatter_sum",
    )(partial)


def adam_update(weight, gradient, first_moment, second_moment):
    first_next = BETA_ONE * first_moment.astype(jnp.float32) + (1.0 - BETA_ONE) * gradient
    second_next = (
        BETA_TWO * second_moment.astype(jnp.float32) + (1.0 - BETA_TWO) * gradient * gradient
    )
    stepped = weight.astype(jnp.float32) - LEARNING_RATE * (first_next * CORRECT_FIRST) / (
        jnp.sqrt(second_next * CORRECT_SECOND) + EPSILON
    )
    return (
        stepped.astype(jnp.bfloat16),
        first_next.astype(jnp.bfloat16),
        second_next.astype(jnp.bfloat16),
    )


def slot_ranks(flat_routes, expert_count):
    onehot = (flat_routes[:, None] == jnp.arange(expert_count, dtype=jnp.int32)[None, :]).astype(
        jnp.int32
    )
    ranks = jnp.cumsum(onehot, axis=0) - 1
    return jnp.sum(ranks * onehot, axis=1)


def in_three(values):
    high = values.astype(jnp.bfloat16)
    rest = values - high.astype(jnp.float32)
    middle = rest.astype(jnp.bfloat16)
    low = (rest - middle.astype(jnp.float32)).astype(jnp.bfloat16)
    return [high, middle, low]


def local(
    tokens,
    routes,
    combine_weight,
    owner_plan,
    w_in,
    w_out,
    grad_in,
    grad_out,
    first_in,
    second_in,
    first_out,
    second_out,
):
    token_count, route_count = routes.shape
    width = tokens.shape[1]
    half = width // 2
    expert_count = owner_plan.shape[0]
    dp = lax.axis_index("dp")
    flat_routes = routes.reshape(-1)
    ranks = slot_ranks(flat_routes, expert_count).reshape(token_count, route_count)
    packed = [routes.astype(jnp.bfloat16), ranks.astype(jnp.bfloat16)] + in_three(combine_weight)
    spare = jnp.zeros((token_count, EXTRA - 5 * route_count), jnp.bfloat16)
    tok = jnp.concatenate([tokens] + packed + [spare], 1)
    grads = jnp.concatenate([grad_in[0], grad_out], 0)
    mine = lax.dynamic_slice_in_dim(grads, dp * half, half, 2)
    other = lax.dynamic_slice_in_dim(grads, (1 - dp) * half, half, 2)
    came = lax.ppermute(other, "dp", [(0, 1), (1, 0)])
    summed = mine.astype(jnp.float32) + came.astype(jnp.float32)
    weights = jnp.concatenate([w_in, w_out[None]], 0)
    firsts = jnp.concatenate([first_in, first_out[None]], 0)
    seconds = jnp.concatenate([second_in, second_out[None]], 0)
    new_w, first_next, second_next = adam_update(weights, summed, firsts, seconds)
    groups = expert_count
    both = jnp.concatenate([first_next.reshape(-1, half), second_next.reshape(-1, half)], 0)
    chunk = both.shape[0] // groups
    spread = lax.all_to_all(
        both.reshape(groups, chunk, half), ("yl", "z", "xh"), 0, 0, tiled=True
    )
    picked = jnp.take(spread, owner_plan, axis=0)
    landed = lax.all_to_all(picked, ("yl", "z", "xh"), 0, 0, tiled=True).reshape(both.shape)
    landed = landed.reshape(2, 3, -1, half)
    all_tok, all_w = gather_all(tok, new_w)
    partial = experts(all_tok, all_w, width, route_count)
    combined = scatter_sum(partial)
    return (
        combined,
        landed[0, :2],
        landed[1, :2],
        landed[0, 2],
        landed[1, 2],
    )


def solution(mesh):
    devices = mesh.devices.reshape(2, 8, 2, 2, 2, 2)
    inner = Mesh(devices, EX + ("dp",))
    both = EX + ("dp",)
    in_specs = (
        P(both, None),
        P(both, None),
        P(both, None),
        P(),
        P(None, EX, "dp"),
        P(EX, "dp"),
        P("dp", None, EX, None),
        P("dp", EX, None),
        P(None, EX, "dp"),
        P(None, EX, "dp"),
        P(EX, "dp"),
        P(EX, "dp"),
    )
    out_specs = (
        P(both, None),
        P(None, EX, "dp"),
        P(None, EX, "dp"),
        P(EX, "dp"),
        P(EX, "dp"),
    )
    return jax.shard_map(local, mesh=inner, in_specs=in_specs, out_specs=out_specs, check_vma=False)
```

time: 806 us -> 428 us (0.53); the launches traced: 794 us -> 427 us
  waiting for transfers between devices: 389 us -> 107 us
  Pallas kernels: 0 us -> 262 us
  local copies, waits for them, and re-layouts: 137 us -> 18.7 us
  matrix products: 69.3 us -> 0 us
  other arithmetic: 69.7 us -> 14.9 us
  starting transfers between devices: 71.1 us -> 23.4 us
  blocking collectives: 42.7 us -> 0 us
  between operations: 14.9 us -> 0.88 us
    pallas_call x0 -> x3, Pallas kernels: none -> 262 us  [the longest x1 155 us: gather_all(): pl.pallas_call(gather_kernel, out_shape=(jax.ShapeDtypeStruct((16, *tok.s...]
    all_to_all x8 -> x2, waiting for transfers between devices: 267 us -> 76 us  [the longest x1 76 us: local(): lax.all_to_all(both.reshape(groups, chunk, half), ('yl', 'z', 'xh'), 0, 0...]
    ppermute x2 -> x1, waiting for transfers between devices: 123 us -> 31.3 us  [local(): came = lax.ppermute(other, 'dp', [(0, 1), (1, 0)])]
    unnamed x39 -> x25, local copies, waits for them, and re-layouts: 80.8 us -> 1.43 us
    dot_general x11 -> x0, matrix products: 69.3 us -> none  [the longest x4 40.9 us: expert_rows(): jnp.dot(hidden, weight_out, preferred_element_type=jnp.float32)]
    all_to_all x8 -> x2, starting transfers between devices: 66 us -> 19.7 us  [the longest x1 12.9 us: local(): lax.all_to_all(both.reshape(groups, chunk, half), ('yl', 'z', 'xh'), 0, 0...]
    all_gather x1 -> x0, blocking collectives: 42.7 us -> none  [local(): lax.all_gather(moved_out, 'dp', axis=1, tiled=True)]
    select_n x8 -> x2, other arithmetic: 30.8 us -> 3.99 us  [local(): picked = jnp.take(spread, owner_plan, axis=0)]
  transfers between devices with their start and end apart: 11 -> 3, of which waited for: 9 -> 2; matrix products, arithmetic and copies ran while one was open for 24% -> 1% of each run, Pallas kernels for 0% -> 61%
where the time goes in v1:
time: 428 us; the launch traced here: 427 us
  Pallas kernels  262 us (61%)
  waiting for transfers between devices  107 us (25%)
  starting transfers between devices  23.4 us (5%)
  local copies, waits for them, and re-layouts  18.7 us (4%)
  other arithmetic  14.9 us (3%)
    pallas_call x1, Pallas kernels, gather_all(): pl.pallas_call(gather_kernel, out_shape=(jax.ShapeDtypeStruct((16, *tok.s...  155 us
    all_to_all x1, waiting for transfers between devices, local(): lax.all_to_all(both.reshape(groups, chunk, half), ('yl', 'z', 'xh'), 0, 0...  76 us
    pallas_call x1, Pallas kernels, scatter_sum(): pl.pallas_call(scatter_kernel, out_shape=jax.ShapeDtypeStruct((t, width),...  62.5 us
    pallas_call x1, Pallas kernels, experts(): pl.pallas_call(functools.partial(moe_kernel, width=width, top=top), out_s...  44.9 us
    ppermute x1, waiting for transfers between devices, local(): came = lax.ppermute(other, 'dp', [(0, 1), (1, 0)])  31.3 us
    all_to_all x1, starting transfers between devices, local(): lax.all_to_all(both.reshape(groups, chunk, half), ('yl', 'z', 'xh'), 0, 0...  12.9 us
  transfers between devices with their start and end apart: 3, of which 2 were waited for; matrix products, arithmetic and copies ran while one was open for 1% of the time, Pallas kernels for 61%

profile of v1, /device:TPU:1, one launch (start us, length us, event | category | flops | bytes accessed | tf_op | source)
XLA Modules:
  0.0 427.3 jit_solution(8583295664924256694)
XLA Ops:
  0.6 0.0 copy-start
  0.6 2.7 fusion.2
  3.3 3.7 collective-permute-start
  7.1 31.3 %collective-permute-done = bf16[3,192,1280]{2,1,0:T(8,128)(2,1)S(1)} collective-permute-done((bf16[3,192,1280]{2,1,0:T(8,128)(2,1)}, bf16[3,192,1280]{2,1,0:T(8,128)(2,1)S(1)}, u32[]{:S(2)}, u32[]{:S(2)}) %collective-permute-start) | collective-permute-done | bytes 1474592 | tf_op jit(solution)/shard_map/ppermute | solution.py:475
  38.4 0.0 copy-done
  38.4 0.0 copy-start.1
  38.4 0.0 copy-start.4
  38.4 0.0 copy-start.6
  38.4 0.0 copy-start.7
  38.4 2.4 fusion.1
  40.8 0.0 copy-done.1
  40.8 0.0 copy-done.2
  40.8 0.0 copy-done.3
  40.8 0.1 copy-done.4
  40.9 0.1 copy-done.6
  41.0 0.1 copy-done.7
  41.2 3.7 fusion.4
  44.8 0.2 pad_maximum_fusion
  45.0 2.4 reshape.52
  47.4 12.9 %all-to-all-start = ((bf16[32,36,1280]{2,1,0:T(8,128)(2,1)}), bf16[32,36,1280]{2,1,0:T(8,128)(2,1)S(1)}, u32[]{:S(2)}, u32[]{:S(2)}) async-start(bf16[32,36,1280]{2,1,0:T(8,128)(2,1)} %reshape.52), calls=%async_computation | async-start | bytes 6553600 | tf_op jit(solution)/shard_map/all_to_all | solution.py:484
  60.3 0.0 copy-done.10
  60.3 76.0 %all-to-all-done = bf16[32,36,1280]{2,1,0:T(8,128)(2,1)S(1)} async-done(((bf16[32,36,1280]{2,1,0:T(8,128)(2,1)}), bf16[32,36,1280]{2,1,0:T(8,128)(2,1)S(1)}, u32[]{:S(2)}, u32[]{:S(2)}) %all-to-all-start) | async-done | bytes 2949152 | tf_op jit(solution)/shard_map/all_to_all | solution.py:484
  136.3 2.4 gather_fusion
  138.8 4.0 broadcast_select_fusion
  142.8 6.8 %all-to-all-start.1 = ((bf16[32,36,1280]{2,1,0:T(8,128)(2,1)}), bf16[32,36,1280]{2,1,0:T(8,128)(2,1)}, u32[]{:S(2)}, u32[]{:S(2)}) async-start(bf16[32,36,1280]{2,1,0:T(8,128)(2,1)} %broadcast_select_fusion), calls=%async_computation.1 | async-start | bytes 6553600 | tf_op jit(solution)/shard_map/all_to_all | solution.py:488
  149.6 0.0 copy-done.9
  149.6 0.1 copy.34
  149.8 0.1 copy.32
  149.9 0.0 copy-done.8
  149.9 0.1 copy.28
  150.0 0.1 eq.29
  150.1 0.1 eq.25
  150.3 0.1 copy.31
  150.4 0.1 copy.33
  150.5 1.7 reduce-window.6
  152.3 0.3 slice_reduce_fusion
  152.6 0.1 fusion.6
  152.7 0.1 convert_element_type.56
  152.9 0.0 copy-done.5
  152.9 1.0 concatenate.18.tok_ref
  153.9 154.6 %gather_all.1 = (bf16[16,128,2688]{2,1,0:T(8,128)(2,1)}, bf16[16,3,192,1280]{3,2,1,0:T(8,128)(2,1)}) custom-call(bf16[128,2688]{1,0:T(8,128)(2,1)} %concatenate.18.tok_ref, bf16[3,192,1280]{2,1,0:T(8,128)(2,1)} %get-tuple-element.12.w_ref), custom_call_target="tpu_custom_call" | custom-call | bytes 400000000 | tf_op jit(solution)/shard_map/gather_all/pallas_call | solution.py:189
  308.6 44.9 %experts.1.p_ref = bf16[16,128,2560]{2,1,0:T(8,128)(2,1)} custom-call(bf16[16,128,2688]{2,1,0:T(8,128)(2,1)} %get-tuple-element.7.tok_ref, bf16[2,2,2,2,576,1280]{5,4,3,2,1,0:T(8,128)(2,1)} %bitcast.31), custom_call_target="tpu_custom_call" | custom-call | flops 12000000000 | bytes 60000000 | tf_op jit(solution)/shard_map/experts/pallas_call | solution.py:295
  353.5 62.5 %scatter_sum.1 = bf16[128,2560]{1,0:T(8,128)(2,1)S(1)} custom-call(bf16[16,128,2560]{2,1,0:T(8,128)(2,1)} %experts.1.p_ref), custom_call_target="tpu_custom_call" | custom-call | bytes 200000000 | tf_op jit(solution)/shard_map/scatter_sum/pallas_call | solution.py:397
  416.0 0.0 all-to-all-done.1
  416.0 5.3 %reshape_reshape.3 = bf16[2,3,192,1280]{3,2,1,0:T(8,128)(2,1)} reshape(bf16[32,36,1280]{2,1,0:T(8,128)(2,1)} %all-to-all-done.1) | data formatting | bytes 5898240 | tf_op jit(solution)/shard_map/reshape;reshape | solution.py:489
  421.3 2.2 slice_bitcast_fusion.2
  423.5 2.9 slice_bitcast_fusion
  426.4 0.8 copy.38
  (16 shorter events, 0.1 us)
Async XLA Ops:
  0.6 37.7 %copy-start = (bf16[1,2,192,2560]{3,2,1,0:T(8,128)(2,1)S(1)}, bf16[1,2,192,2560]{3,2,1,0:T(8,128)(2,1)}, u32[]{:S(2)}) copy-start(bf16[1,2,192,2560]{3,2,1,0:T(8,128)(2,1)} %param.18) | copy-start | bytes 5898244
  3.3 35.0 %collective-permute-start = (bf16[3,192,1280]{2,1,0:T(8,128)(2,1)}, bf16[3,192,1280]{2,1,0:T(8,128)(2,1)S(1)}, u32[]{:S(2)}, u32[]{:S(2)}) collective-permute-start(bf16[3,192,1280]{2,1,0:T(8,128)(2,1)} %fusion.2), channel_id=1, source_target_pairs={{0,1},{1,0},{2,3},{3,2},{4,5},{5,4},{6,7},{7,6},{8,9},{9,8},{10,11... | collective-permute-start | bytes 4423688 | tf_op jit(solution)/shard_map/ppermute | solution.py:475
  38.4 2.4 copy-start.1
  38.4 2.5 copy-start.2
  38.4 2.5 copy-start.3
  38.4 2.5 copy-start.4
  38.4 2.6 copy-start.6
  38.4 2.8 copy-start.7
  47.4 12.9 %copy-start.10 = (s32[32]{0:T(128)S(1)}, s32[32]{0:T(128)}, u32[]{:S(2)}) copy-start(s32[32]{0:T(128)} %param.15) | copy-start | bytes 388
  47.4 88.9 %all-to-all-start = ((bf16[32,36,1280]{2,1,0:T(8,128)(2,1)}), bf16[32,36,1280]{2,1,0:T(8,128)(2,1)S(1)}, u32[]{:S(2)}, u32[]{:S(2)}) async-start(bf16[32,36,1280]{2,1,0:T(8,128)(2,1)} %reshape.52), calls=%async_computation | async-start | bytes 6553600 | tf_op jit(solution)/shard_map/all_to_all | solution.py:484
  142.8 6.8 %copy-start.9 = (f32[128,6]{0,1:T(8,128)S(1)}, f32[128,6]{0,1:T(8,128)}, u32[]{:S(2)}) copy-start(f32[128,6]{0,1:T(8,128)} %param.14) | copy-start | bytes 9220
  142.8 7.1 %copy-start.8 = (s32[128,6]{0,1:T(8,128)S(1)}, s32[128,6]{0,1:T(8,128)}, u32[]{:S(2)}) copy-start(s32[128,6]{0,1:T(8,128)} %param.13) | copy-start | bytes 9220
  142.8 10.1 %copy-start.5 = (bf16[128,2560]{1,0:T(8,128)(2,1)S(1)}, bf16[128,2560]{1,0:T(8,128)(2,1)}, u32[]{:S(2)}) copy-start(bf16[128,2560]{1,0:T(8,128)(2,1)} %param.12) | copy-start | bytes 1966084
  142.8 273.2 %all-to-all-start.1 = ((bf16[32,36,1280]{2,1,0:T(8,128)(2,1)}), bf16[32,36,1280]{2,1,0:T(8,128)(2,1)}, u32[]{:S(2)}, u32[]{:S(2)}) async-start(bf16[32,36,1280]{2,1,0:T(8,128)(2,1)} %broadcast_select_fusion), calls=%async_computation.1 | async-start | bytes 6553600 | tf_op jit(solution)/shard_map/all_to_all | solution.py:488
